TPU v7x, 256 devices: a whole 4x4x8 slice. The times are simulated.
256 devices in a mesh: epoch: 64 (over y, z, x_lo), blend: 4 (over x_hi, core).
Axes of the slice: x: 4 (x_hi: 2, x_lo: 2; x = x_hi * 2 + x_lo), y: 4, z: 8, core: 2. Of those that a mesh axis runs over, the one named last changes fastest.
Arguments:
- models: float32 [4, 128, 6, 4096], P('blend', 'epoch'), may hold values from -6 to 6
- observed: bfloat16 [64, 512, 4096], P('epoch', 'blend'), may hold values from -6 to 6
- weights: float32 [64, 512], P('epoch', 'blend'), may hold values from 0.5 to 2
- coverage: int32 [64, 512], P('epoch', 'blend'), may hold values from 0 to 1, as said below
- offsets: int32 [64, 512, 2], P('epoch', 'blend'), may hold values from 0 to 63
- counts: int32 [4, 128], P('blend', 'epoch'), may hold values from 1 to 64, as said below
- psf_y: bfloat16 [64, 4096], P('epoch'), may hold values from -0.75 to 0.75
- resample_y: bfloat16 [64, 4096], P('epoch'), may hold values from -0.75 to 0.75
- psf_x: bfloat16 [64, 4096], P('epoch'), may hold values from -0.75 to 0.75
- resample_x: bfloat16 [64, 4096], P('epoch'), may hold values from -0.75 to 0.75
Outputs:
- updated: float32 [4, 128, 6, 4096], P('blend', 'epoch')
Inputs may be any that keep to these rules, and one draw needn't show every extreme that they name: `coverage`: every blend is seen by one epoch or more. counts of blend b is the sum of coverage over all epochs for b.
All inputs are finite; a program needn't handle non-finite values.
Results may differ from a plain program's by a relative error of at most 0.0017.
Values may be sent and summed in bfloat16 or wider, within the bound.
A program may use at most 128 MiB of HBM per device.

v0:
```python
import jax
import jax.numpy as jnp
from jax import lax
from jax.sharding import PartitionSpec as P

CUT = 64
BANDS = 6
PIX2 = 4096


step_size = 0.5


def roll_forward(image, down, across):
    side = image.shape[0]
    doubled = jnp.concatenate([image, image], axis=0)
    rows = lax.dynamic_slice_in_dim(doubled, down, side, 0)
    doubled = jnp.concatenate([rows, rows], axis=1)
    return lax.dynamic_slice_in_dim(doubled, across, side, 1)


def one_epoch(model_low, observed, scale, offsets, left, right, band):
    side = left.shape[0]
    count = observed.shape[0]
    chosen = lax.dynamic_index_in_dim(model_low, band, 1, keepdims=False)
    shifted = jax.vmap(roll_forward)(chosen, offsets[:, 0], offsets[:, 1])
    blurred = jnp.einsum("ij,bjk->bik", left, shifted, preferred_element_type=jnp.float32).astype(
        jnp.bfloat16
    )
    predicted = jnp.einsum("bik,lk->bil", blurred, right, preferred_element_type=jnp.float32)
    target = observed.reshape(count, side, side).astype(jnp.float32)
    misfit = (scale[:, None, None] * (predicted - target)).astype(jnp.bfloat16)
    back = jnp.einsum("ji,bjk->bik", left, misfit, preferred_element_type=jnp.float32).astype(
        jnp.bfloat16
    )
    term = jnp.einsum("bik,kl->bil", back, right, preferred_element_type=jnp.float32)
    return jax.vmap(roll_forward)(term, side - offsets[:, 0], side - offsets[:, 1])


def on_device(
    models, observed, weights, coverage, offsets, counts, psf_y, resample_y, psf_x, resample_x
):
    ep_dev = observed.shape[0]
    group_size = lax.axis_size("epoch")
    all_epochs = ep_dev * group_size
    anchor = lax.axis_index("epoch") * ep_dev
    lefts = jnp.einsum(
        "eij,ejk->eik",
        psf_y.reshape(ep_dev, CUT, CUT),
        resample_y.reshape(ep_dev, CUT, CUT),
        preferred_element_type=jnp.float32,
    ).astype(jnp.bfloat16)
    rights = jnp.einsum(
        "eij,ejk->eik",
        psf_x.reshape(ep_dev, CUT, CUT),
        resample_x.reshape(ep_dev, CUT, CUT),
        preferred_element_type=jnp.float32,
    ).astype(jnp.bfloat16)
    scale = weights * coverage.astype(jnp.float32)
    epoch_bands = (anchor + 0) * BANDS // all_epochs
    first_band = anchor * BANDS // all_epochs
    model_low = models.astype(jnp.bfloat16)
    piece = lax.all_gather(model_low, "epoch", axis=1, tiled=True)
    count = piece.shape[1]
    blocks = piece[0].reshape(count, BANDS, CUT, CUT)
    terms = one_epoch(
        blocks, observed[0], scale[0], offsets[0], lefts[0], rights[0], epoch_bands
    ).reshape(count, PIX2)
    total = jnp.zeros((count, 2, PIX2), jnp.float32)
    slot = epoch_bands - first_band
    current = lax.dynamic_index_in_dim(total, slot, 1, keepdims=False)
    total = lax.dynamic_update_index_in_dim(total, current + terms, slot, 1)
    received = lax.all_to_all(total, "epoch", split_axis=0, concat_axis=1, tiled=True)
    slot_count = received.shape[1]
    position = jnp.arange(slot_count, dtype=jnp.int32)
    source = position // 2
    band_of = source * ep_dev * BANDS // all_epochs + position % 2
    selector = (band_of[:, None] == jnp.arange(BANDS, dtype=jnp.int32)[None, :]).astype(jnp.float32)
    gradient = jnp.einsum("bkp,kc->bcp", received, selector, precision=lax.Precision.HIGHEST)
    divisor = counts[0].astype(jnp.float32)[:, None, None]
    updated = models[0] - step_size * gradient / divisor
    return updated[None]


def solution(mesh):
    return jax.shard_map(
        on_device,
        mesh=mesh,
        in_specs=(
            P("blend", "epoch", None, None),
            P("epoch", "blend", None),
            P("epoch", "blend"),
            P("epoch", "blend"),
            P("epoch", "blend", None),
            P("blend", "epoch"),
            P("epoch", None),
            P("epoch", None),
            P("epoch", None),
            P("epoch", None),
        ),
        out_specs=P("blend", "epoch", None, None),
        check_vma=False,
    )
```

profile of v0, /device:TPU:4, one launch (start us, length us, event | category | flops | bytes accessed | tf_op | source)
XLA Modules:
  0.0 520.7 jit_solution(16217948494286441168)
XLA Ops:
  11.7 2.3 copy.55
  15.7 308.8 %all-gather.2.cloned.1.call-done = bf16[1,128,6,4096]{3,2,0,1:T(8,128)(2,1)} async-done(((bf16[1,2,6,4096]{3,2,0,1:T(8,128)(2,1)}), bf16[1,128,6,4096]{3,2,0,1:T(8,128)(2,1)}) %all-gather.2.cloned.1.call-update) | async-done | bytes 6291472 | tf_op jit(solution)/shard_map/all_gather | solution.py:63
  324.5 11.1 %copy.50 = bf16[1,128,6,4096]{1,3,2,0:T(8,128)(2,1)} copy(bf16[1,128,6,4096]{3,2,0,1:T(8,128)(2,1)} %all-gather.2.cloned.1.call-done) | data formatting | bytes 12582912 | tf_op jit(solution)/shard_map/all_gather | solution.py:63
  338.0 2.7 pad_maximum_fusion
  340.7 8.5 %gather_fusion = bf16[128,64,64]{2,0,1:T(8,128)(2,1)S(1)} fusion(bf16[128,128,64]{2,0,1:T(8,128)(2,1)} %pad_maximum_fusion, s32[128]{0:T(128)S(1)} %get-tuple-element.6), kind=kCustom, calls=%fused_computation | custom fusion | bytes 2098688 | tf_op jit(solution)/shard_map/vmap()/gather | solution.py:17
  349.3 2.5 pad_maximum_fusion.3
  351.8 9.0 %copy.52 = bf16[128,64,128]{1,0,2:T(8,128)(2,1)} copy(bf16[128,64,128]{2,0,1:T(8,128)(2,1)} %pad_maximum_fusion.3) | data formatting | bytes 4194304 | tf_op jit(solution)/shard_map/vmap()/concatenate | solution.py:18
  360.8 8.5 %gather_fusion.1 = bf16[128,64,64]{1,0,2:T(8,128)(2,1)S(1)} fusion(bf16[128,64,128]{1,0,2:T(8,128)(2,1)} %copy.52, s32[128]{0:T(128)S(1)} %get-tuple-element.7), kind=kCustom, calls=%fused_computation.1 | custom fusion | bytes 2098688 | tf_op jit(solution)/shard_map/vmap()/gather | solution.py:19
  369.3 3.6 convert_bitcast_fusion
  373.0 4.5 copy.54
  379.7 2.7 pad_maximum_fusion.1
  382.5 7.1 %copy.60 = f32[128,128,64]{2,0,1:T(8,128)} copy(f32[128,128,64]{0,2,1:T(8,128)} %pad_maximum_fusion.1) | data formatting | bytes 8388608 | tf_op jit(solution)/shard_map/vmap()/concatenate | solution.py:16
  389.6 9.9 %gather_fusion.2 = f32[128,64,64]{2,0,1:T(8,128)} fusion(f32[128,128,64]{2,0,1:T(8,128)} %copy.60, s32[128]{0:T(128)S(1)} %get-tuple-element.8), kind=kCustom, calls=%fused_computation.2 | custom fusion | bytes 4195840 | tf_op jit(solution)/shard_map/vmap()/gather | solution.py:17
  399.5 6.6 %pad_maximum_fusion.2 = f32[128,64,128]{2,0,1:T(8,128)} fusion(f32[128,64,64]{2,0,1:T(8,128)} %gather_fusion.2), kind=kLoop, calls=%fused_computation.11 | loop fusion | flops 1048576 | bytes 6291456 | tf_op jit(solution)/shard_map/vmap()/concatenate | solution.py:18
  406.1 9.2 %copy.61 = f32[128,64,128]{1,0,2:T(8,128)} copy(f32[128,64,128]{2,0,1:T(8,128)} %pad_maximum_fusion.2) | data formatting | bytes 8388608 | tf_op jit(solution)/shard_map/vmap()/concatenate | solution.py:18
  415.3 9.9 %gather_fusion.3 = f32[128,64,64]{1,0,2:T(8,128)} fusion(f32[128,64,128]{1,0,2:T(8,128)} %copy.61, s32[128]{0:T(128)S(1)} %get-tuple-element.5), kind=kCustom, calls=%fused_computation.3 | custom fusion | bytes 4195840 | tf_op jit(solution)/shard_map/vmap()/gather | solution.py:19
  425.2 4.2 copy.62
  429.4 5.1 copy.70
  434.5 3.9 dynamic_update_slice.4.clone
  438.4 6.6 %all-to-all-start = ((f32[128,2,4096]{2,1,0:T(2,128)}), f32[128,2,4096]{2,1,0:T(2,128)}, u32[]{:S(2)}, u32[]{:S(2)}) async-start(f32[128,2,4096]{2,1,0:T(2,128)} %dynamic_update_slice.4.clone), calls=%async_computation | async-start | bytes 8388608 | tf_op jit(solution)/shard_map/all_to_all | solution.py:73
  445.0 53.0 %all-to-all-done = f32[128,2,4096]{2,1,0:T(2,128)} async-done(((f32[128,2,4096]{2,1,0:T(2,128)}), f32[128,2,4096]{2,1,0:T(2,128)}, u32[]{:S(2)}, u32[]{:S(2)}) %all-to-all-start) | async-done | bytes 4194336 | tf_op jit(solution)/shard_map/all_to_all | solution.py:73
  498.0 4.7 copy.64
  502.8 6.1 %all_to_all.16 = f32[2,128,4096]{2,1,0:T(8,128)} reshape(f32[2,64,2,4096]{3,2,1,0:T(2,128)} %copy.64) | data formatting | bytes 8388608 | tf_op jit(solution)/shard_map/all_to_all | solution.py:73
  508.9 3.7 fusion.3
  (30 shorter events, 12.3 us)
Async XLA Ops:
  6.5 317.9 %all-gather.2.cloned.1.call-start = ((), (), s32[]{:S(2)}) async-start(), calls=%async_computation.1 | async-start | bytes 8519680 | tf_op jit(solution)/shard_map/all_gather | solution.py:63
  369.3 8.2 %copy-start = (bf16[1,128,4096]{1,2,0:T(8,128)(2,1)S(1)}, bf16[1,128,4096]{1,2,0:T(8,128)(2,1)}, u32[]{:S(2)}) copy-start(bf16[1,128,4096]{1,2,0:T(8,128)(2,1)} %copy.55) | copy-start | bytes 3145732
  438.4 6.6 %copy-start.2 = (s32[1,2]{1,0:T(1,128)S(1)}, s32[1,2]{1,0:T(1,128)}, u32[]{:S(2)}) copy-start(s32[1,2]{1,0:T(1,128)} %param.15) | copy-start | bytes 28
  438.4 59.6 %all-to-all-start = ((f32[128,2,4096]{2,1,0:T(2,128)}), f32[128,2,4096]{2,1,0:T(2,128)}, u32[]{:S(2)}, u32[]{:S(2)}) async-start(f32[128,2,4096]{2,1,0:T(2,128)} %dynamic_update_slice.4.clone), calls=%async_computation | async-start | bytes 8388608 | tf_op jit(solution)/shard_map/all_to_all | solution.py:73
  502.8 6.1 %copy-start.1 = (f32[1,2,6,4096]{3,1,2,0:T(2,128)S(1)}, f32[1,2,6,4096]{3,1,2,0:T(2,128)}, u32[]{:S(2)}) copy-start(f32[1,2,6,4096]{3,1,2,0:T(2,128)} %param.10) | copy-start | bytes 589828
Sparse Core Ops, SparseCore 0:
  9.1 315.3 all-gather.1
where the time goes:
time: 529 us; the launch traced here: 521 us
  waiting for transfers between devices  362 us (68%)
  local copies, waits for them, and re-layouts  108 us (20%)
  other arithmetic  20.1 us (4%)
  between operations  14 us (3%)
  matrix products  9.81 us (2%)
  starting transfers between devices  6.56 us (1%)
    all_gather x1, waiting for transfers between devices, on_device(): piece = lax.all_gather(model_low, 'epoch', axis=1, tiled=True)  309 us
    all_to_all x1, waiting for transfers between devices, on_device(): lax.all_to_all(total, 'epoch', split_axis=0, concat_axis=1, tiled=True)  53 us
    gather x3, local copies, waits for them, and re-layouts, roll_forward(): return lax.dynamic_slice_in_dim(doubled, across, side, 1)  22.7 us
    gather x2, local copies, waits for them, and re-layouts, roll_forward(): rows = lax.dynamic_slice_in_dim(doubled, down, side, 0)  18.5 us
    concatenate x2, local copies, waits for them, and re-layouts, roll_forward(): doubled = jnp.concatenate([rows, rows], axis=1)  18.2 us
    all_gather x1, local copies, waits for them, and re-layouts, on_device(): piece = lax.all_gather(model_low, 'epoch', axis=1, tiled=True)  11.1 us
    all_to_all x2, local copies, waits for them, and re-layouts, on_device(): lax.all_to_all(total, 'epoch', split_axis=0, concat_axis=1, tiled=True)  10.8 us
  transfers between devices with their start and end apart: 2, of which 2 were waited for; matrix products, arithmetic and copies ran while one was open for 1% of the time, Pallas kernels for 0%

commit v1 on v0

v1 whole, which is shorter than its diff:
```python
import functools

import jax
import jax.numpy as jnp
from jax import lax
from jax.experimental import pallas as pl
from jax.experimental.pallas import tpu as pltpu
from jax.sharding import PartitionSpec as P

CUT = 64
BANDS = 6
PIX2 = 4096
E = 64
NY, NZ = 4, 8
step_size = 0.5
MESH = pl.DeviceIdType.MESH
F32, BF16 = jnp.float32, jnp.bfloat16


def band_of(epoch):
    return epoch * BANDS // E


STRADDLERS = [
    (y, z) for y in range(NY) for z in range(NZ) if band_of((y * NZ + z) * 2) != band_of((y * NZ + z) * 2 + 1)
]


def kernel(
    models, obs_hbm, weights, coverage, offs, counts, psf_y, res_y, psf_x, res_x, out,
    obs_v, obs_st, obs_in, models_low, mod_in, term_out, term_out2, term_in, term_in2,
    mats, mats_in, tab_a, tab_at, tab_r, fold, rows_f, wide, spread,
    scale_v, scale_in, offs_in, off_own, off_par, sc_own, sc_par,
    in_s, in_r, in2_s, in2_r, obs_s, obs_r, t_s, t_r, t2_s, t2_r, small_s, small_r, local,
):
    me = lax.axis_index("epoch")
    x = lax.rem(me, 2)
    z = lax.rem(lax.div(me, 2), NZ)
    y = lax.div(me, 2 * NZ)
    partner = me + 1 - 2 * x

    def device(yy, zz):
        return (yy * NZ + zz) * 2 + x

    def place(ky, kz):
        return lax.rem(y + ky, NY), lax.rem(z + kz, NZ)

    relative = [(ky, kz) for kz in (4, 3, 5, 2, 6, 1, 7, 0) for ky in (2, 1, 3, 0)]
    others = [r for r in relative if r != (0, 0)]

    def remote(src, dst, send, recv, target):
        return pltpu.make_async_remote_copy(
            src_ref=src, dst_ref=dst, send_sem=send, recv_sem=recv, device_id={"epoch": target}, device_id_type=MESH
        )

    barrier = pltpu.get_barrier_semaphore()
    pl.semaphore_signal(barrier, inc=1, device_id={"epoch": partner}, device_id_type=MESH)
    for ky, kz in others:
        pl.semaphore_signal(barrier, inc=1, device_id={"epoch": device(*place(ky, kz))}, device_id_type=MESH)

    load_obs = pltpu.make_async_copy(obs_hbm, obs_v, local.at[0])
    load_obs.start()
    load_off = pltpu.make_async_copy(offs, off_own, local.at[1])
    load_off.start()
    scale_v[...] = weights[...] * coverage[...].astype(F32)

    straddle = jnp.int32(0)
    straddle_id = jnp.int32(0)
    for i, (ys, zs) in enumerate(STRADDLERS):
        hit = jnp.where(jnp.logical_and(y == ys, z == zs), 1, 0).astype(jnp.int32)
        straddle = straddle + hit
        straddle_id = straddle_id + i * hit

    lane = lax.broadcasted_iota(jnp.int32, (CUT, 128), 1)
    row = lax.broadcasted_iota(jnp.int32, (CUT, 128), 0)
    low = lane < CUT
    low_half = low[:32]
    even = lax.rem(row, 2) == 0
    mask_lo = jnp.where(low, 1.0, 0.0).astype(BF16)
    mask_hi = jnp.where(low, 0.0, 1.0).astype(BF16)

    def swap(v):
        turned = pltpu.roll(v, CUT, 1)
        up = pltpu.roll(turned, CUT - 1, 0)
        down = pltpu.roll(turned, 1, 0)
        return jnp.where(low, jnp.where(even, v, down), jnp.where(even, up, v))

    def unfold(ref):
        v = ref[...].astype(F32)
        for k in range(32):
            fold[k : k + 1, :] = v[:, k * 128 : (k + 1) * 128]
        top = fold[...]
        return top, pltpu.roll(top, CUT, 1)

    def natural(ref):
        top, bottom = unfold(ref)
        rows_f[pl.ds(0, 32, stride=2), :] = top
        rows_f[pl.ds(1, 32, stride=2), :] = bottom
        return rows_f[...]

    def doubled(v):
        return jnp.where(low, v, pltpu.roll(v, CUT, 1))

    top, bottom = unfold(psf_y)
    first = jnp.concatenate([top, bottom], axis=0)[:, :CUT].astype(BF16)
    second = doubled(natural(res_y)).astype(BF16)
    mats[0] = jnp.dot(first, second, preferred_element_type=F32).astype(BF16)
    first = natural(psf_x)[:, :CUT].astype(BF16)
    second = doubled(natural(res_x)).astype(BF16)
    mats[1] = jnp.dot(first, second, preferred_element_type=F32).astype(BF16)

    for c in range(BANDS):
        models_low[c] = swap(models[c]).astype(BF16)

    def tables(slot, source):
        left = source[0].astype(F32)
        right = source[1].astype(F32)
        wide[...] = jnp.concatenate([left, left], axis=0).T

        def one(d, carry):
            tab_a[slot, d] = pltpu.roll(left, d, 1).astype(BF16)
            tab_at[slot, d] = wide[pl.ds(CUT - d, CUT), :].astype(BF16)
            tab_r[slot, d] = pltpu.roll(right, d, 1).astype(BF16)
            return carry

        lax.fori_loop(0, CUT, one, 0, unroll=4)

    load_obs.wait()

    def relayout(m, carry):
        spread[...] = obs_v[m].astype(F32)
        yy = lax.div(m, 4)
        z2 = 2 * lax.rem(m, 4)
        for s in range(4):
            f0 = spread[pl.ds(2 * s, 32, stride=8), :]
            f1 = spread[pl.ds(2 * s + 1, 32, stride=8), :]
            top = jnp.where(low_half, f0, pltpu.roll(f1, CUT, 1))
            bottom = jnp.where(low_half, pltpu.roll(f0, CUT, 1), f1)
            obs_st[s % 2, z2 + s // 2, yy] = jnp.concatenate([top, bottom], axis=0).astype(BF16)
        return carry

    lax.fori_loop(0, 16, relayout, 0)

    load_off.wait()
    load_scale = pltpu.make_async_copy(scale_v, sc_own, local.at[2])
    load_scale.start()
    load_scale.wait()

    pl.semaphore_wait(barrier, 32)

    send_mats = remote(mats, mats_in, small_s.at[0], small_r.at[0], partner)
    send_off = remote(offs, offs_in, small_s.at[1], small_r.at[1], partner)
    send_scale = remote(scale_v, scale_in, small_s.at[2], small_r.at[2], partner)
    send_mats.start()
    send_off.start()
    send_scale.start()

    def obs_copy(g):
        zz = lax.rem(z + far_first(g), NZ)
        return remote(obs_st.at[1 - x, zz], obs_in.at[zz], obs_s.at[g], obs_r.at[g], partner)

    def far_first(g):
        return 4 + lax.div(g + 1, 2) * (1 - 2 * lax.rem(g, 2))

    for g in range(8):
        obs_copy(jnp.int32(g)).start()

    def model_copy(ky, kz):
        yy, zz = place(ky, kz)
        band = lax.div((yy * NZ + zz) * 2 * BANDS, E)
        return remote(
            models_low.at[band], mod_in.at[0, z, y], in_s.at[zz * NY + yy], in_r.at[z * NY + y], device(yy, zz)
        )

    for ky, kz in others:
        model_copy(ky, kz).start()
    for i, (ys, zs) in enumerate(STRADDLERS):
        band = band_of((ys * NZ + zs) * 2 + 1)
        here = jnp.logical_and(y == ys, z == zs)

        @pl.when(jnp.logical_not(here))
        def _():
            remote(
                models_low.at[band], mod_in.at[1, z, y], in2_s.at[i], in2_r.at[z * NY + y], device(ys, zs)
            ).start()

        @pl.when(here)
        def _():
            mod_in[1, z, y] = models_low[band]

    mod_in[0, z, y] = models_low[lax.div((y * NZ + z) * 2 * BANDS, E)]

    tables(0, mats)
    send_mats.wait_recv()
    tables(1, mats_in)
    send_off.wait_recv()
    send_scale.wait_recv()
    load_off = pltpu.make_async_copy(offs_in, off_par, local.at[3])
    load_scale = pltpu.make_async_copy(scale_in, sc_par, local.at[4])
    load_off.start()
    load_scale.start()
    load_off.wait()
    load_scale.wait()

    slot_own = straddle * x
    slot_par = straddle * (1 - x)
    own_first = slot_own == 0
    par_first = slot_par == 0
    offsets = (off_own, off_par)
    scales = (sc_own, sc_par)

    def term_copy(yy, zz):
        return remote(
            term_out.at[zz, yy], term_in.at[z, y], t_s.at[zz * NY + yy], t_r.at[z * NY + y], device(yy, zz)
        )

    def term2_copy(yy, zz):
        return remote(
            term_out2.at[zz, yy], term_in2.at[straddle_id], t2_s.at[zz * NY + yy], t2_r.at[straddle_id], device(yy, zz)
        )

    def split(v):
        return jnp.concatenate([v * mask_lo, v * mask_hi], axis=0)

    def group(g, carry):
        zz = lax.rem(z + far_first(g), NZ)
        obs_copy(g).wait_recv()
        units = []
        for ky in (2, 1, 3, 0):
            yy = lax.rem(y + ky, NY)

            def arrive():
                slot = zz * NY + yy
                remote(models_low.at[0], mod_in.at[0, zz, yy], in_s.at[slot], in_r.at[slot], partner).wait_recv()

                @pl.when(straddle == 1)
                def _():
                    remote(models_low.at[0], mod_in.at[1, zz, yy], in_s.at[slot], in2_r.at[slot], partner).wait_recv()

            if ky == 0:
                pl.when(g < 7)(arrive)
            else:
                arrive()
            for e in range(2):
                units.append((yy, e))
        state = []
        for yy, e in units:
            b = 2 * ((yy * NZ + zz) * 2 + x)
            dy0, dx0 = offsets[e][0, b], offsets[e][1, b]
            dy1, dx1 = offsets[e][0, b + 1], offsets[e][1, b + 1]
            left = tab_a[e, dy0] * mask_lo + tab_a[e, dy1] * mask_hi
            image = mod_in[slot_own if e == 0 else slot_par, zz, yy]
            blurred = jnp.dot(left, split(image), preferred_element_type=F32).astype(BF16)
            state.append([yy, e, b, dy0, dy1, dx0, dx1, blurred])
        for s in state:
            yy, e, b, dy0, dy1, dx0, dx1, blurred = s
            right = jnp.concatenate([tab_r[e, dx0] * mask_lo, tab_r[e, dx1] * mask_hi], axis=0)
            predicted = lax.dot_general(blurred, right, (((1,), (1,)), ((), ())), preferred_element_type=F32)
            seen = (obs_st[x, zz, yy] if e == 0 else obs_in[zz, yy]).astype(F32)
            scale = jnp.where(low[:1], scales[e][0, b], scales[e][0, b + 1])
            s.append((scale * (predicted - seen)).astype(BF16))
        for s in state:
            yy, e, b, dy0, dy1, dx0, dx1, blurred, misfit = s
            left_t = tab_at[e, dy0] * mask_lo + tab_at[e, dy1] * mask_hi
            s.append(jnp.dot(left_t, split(misfit), preferred_element_type=F32).astype(BF16))
        terms = {}
        for s in state:
            yy, e, b, dy0, dy1, dx0, dx1, blurred, misfit, back = s
            right = jnp.concatenate([tab_r[e, dx0] * mask_lo, tab_r[e, dx1] * mask_hi], axis=0)
            terms.setdefault(len(terms) if e == 0 else len(terms) - 1, [yy]).append(
                jnp.dot(back, right, preferred_element_type=F32)
            )
        for yy, own, par in terms.values():
            zero = jnp.zeros_like(own)
            term_out[zz, yy] = (jnp.where(own_first, own, zero) + jnp.where(par_first, par, zero)).astype(BF16)
            term_out2[zz, yy] = (jnp.where(own_first, zero, own) + jnp.where(par_first, zero, par)).astype(BF16)
        for ky in (2, 1, 3, 0):
            yy = lax.rem(y + ky, NY)

            def ship():
                term_copy(yy, zz).start()

                @pl.when(straddle == 1)
                def _():
                    term2_copy(yy, zz).start()

            if ky == 0:
                pl.when(g < 7)(ship)
            else:
                ship()
        return carry

    lax.fori_loop(0, 8, group, 0)

    term_in[z, y] = term_out[z, y]

    @pl.when(straddle == 1)
    def _():
        term_in2[straddle_id] = term_out2[z, y]

    for ky, kz in others:
        yy, zz = place(ky, kz)
        slot = zz * NY + yy
        remote(term_out.at[zz, yy], term_in.at[zz, yy], t_s.at[slot], t_r.at[slot], partner).wait_recv()
    for i, (ys, zs) in enumerate(STRADDLERS):

        @pl.when(jnp.logical_not(jnp.logical_and(y == ys, z == zs)))
        def _():
            remote(term_out2.at[0, 0], term_in2.at[i], t2_s.at[0], t2_r.at[i], partner).wait_recv()

    seen_by = jnp.where(even, counts[0, 0].astype(F32), counts[0, 1].astype(F32))
    factor = step_size / seen_by
    for c in range(BANDS):
        total = jnp.zeros((CUT, 128), F32)
        for yy in range(NY):
            for zz in range(NZ):
                if band_of((yy * NZ + zz) * 2) == c:
                    total = total + term_in[zz, yy].astype(F32)
        for i, (ys, zs) in enumerate(STRADDLERS):
            if band_of((ys * NZ + zs) * 2 + 1) == c:
                total = total + term_in2[i].astype(F32)
        out[c] = models[c] - factor * swap(total)

    send_mats.wait_send()
    send_off.wait_send()
    send_scale.wait_send()
    for g in range(8):
        obs_copy(jnp.int32(g)).wait_send()
    for ky, kz in others:
        model_copy(ky, kz).wait_send()
        yy, zz = place(ky, kz)
        term_copy(yy, zz).wait_send()

        @pl.when(straddle == 1)
        def _():
            term2_copy(yy, zz).wait_send()

    for i, (ys, zs) in enumerate(STRADDLERS):

        @pl.when(jnp.logical_not(jnp.logical_and(y == ys, z == zs)))
        def _():
            remote(models_low.at[0], mod_in.at[1, z, y], in2_s.at[i], in2_r.at[0], partner).wait_send()


def on_device(
    models, observed, weights, coverage, offsets, counts, psf_y, resample_y, psf_x, resample_x
):
    pair_models = models[0].reshape(2, BANDS, 32, 128).transpose(1, 2, 0, 3).reshape(BANDS, CUT, 128)
    blocks = observed[0].reshape(16, 8, 32, 128).transpose(0, 2, 1, 3).reshape(16, 256, 128)
    vmem = pl.BlockSpec(memory_space=pltpu.VMEM)
    dma = pltpu.SemaphoreType.DMA
    updated = pl.pallas_call(
        kernel,
        out_shape=jax.ShapeDtypeStruct((BANDS, CUT, 128), F32),
        in_specs=[
            vmem, pl.BlockSpec(memory_space=pl.ANY), vmem, vmem, vmem, pl.BlockSpec(memory_space=pltpu.SMEM),
            vmem, vmem, vmem, vmem,
        ],
        out_specs=vmem,
        scratch_shapes=[
            pltpu.VMEM((16, 256, 128), BF16),
            pltpu.VMEM((2, NZ, NY, CUT, 128), BF16),
            pltpu.VMEM((NZ, NY, CUT, 128), BF16),
            pltpu.VMEM((BANDS, CUT, 128), BF16),
            pltpu.VMEM((2, NZ, NY, CUT, 128), BF16),
            pltpu.VMEM((NZ, NY, CUT, 128), BF16),
            pltpu.VMEM((NZ, NY, CUT, 128), BF16),
            pltpu.VMEM((NZ, NY, CUT, 128), BF16),
            pltpu.VMEM((len(STRADDLERS), CUT, 128), BF16),
            pltpu.VMEM((2, CUT, 128), BF16),
            pltpu.VMEM((2, CUT, 128), BF16),
            pltpu.VMEM((2, CUT, CUT, 128), BF16),
            pltpu.VMEM((2, CUT, CUT, 128), BF16),
            pltpu.VMEM((2, CUT, CUT, 128), BF16),
            pltpu.VMEM((32, 128), F32),
            pltpu.VMEM((CUT, 128), F32),
            pltpu.VMEM((128, 128), F32),
            pltpu.VMEM((256, 128), F32),
            pltpu.VMEM((1, 128), F32),
            pltpu.VMEM((1, 128), F32),
            pltpu.VMEM((2, 128), jnp.int32),
            pltpu.SMEM((2, 128), jnp.int32),
            pltpu.SMEM((2, 128), jnp.int32),
            pltpu.SMEM((1, 128), F32),
            pltpu.SMEM((1, 128), F32),
            dma((32,)), dma((32,)), dma((2,)), dma((32,)), dma((8,)), dma((8,)),
            dma((32,)), dma((32,)), dma((32,)), dma((2,)), dma((3,)), dma((3,)), dma((5,)),
        ],
        compiler_params=pltpu.CompilerParams(
            collective_id=0, has_side_effects=True, vmem_limit_bytes=48 * 2**20
        ),
    )(
        pair_models, blocks, weights, coverage, offsets[0].T, counts, psf_y, resample_y, psf_x, resample_x
    )
    return updated.reshape(BANDS, 32, 2, 128).transpose(2, 0, 1, 3).reshape(1, 2, BANDS, PIX2)


def solution(mesh):
    return jax.shard_map(
        on_device,
        mesh=mesh,
        in_specs=(
            P("blend", "epoch", None, None),
            P("epoch", "blend", None),
            P("epoch", "blend"),
            P("epoch", "blend"),
            P("epoch", "blend", None),
            P("blend", "epoch"),
            P("epoch", None),
            P("epoch", None),
            P("epoch", None),
            P("epoch", None),
        ),
        out_specs=P("blend", "epoch", None, None),
        check_vma=False,
    )
```

time: 529 us -> 49.7 us (0.09)
  the two profiles are of different devices: /device:TPU:4 before, /device:TPU:100 now
where the time goes in v1:
time: 49.7 us; the launch traced here: 49.3 us
  Pallas kernels  42.8 us (86%)
  local copies, waits for them, and re-layouts  6.4 us (13%)
    pallas_call x1, Pallas kernels, on_device(): pl.pallas_call(kernel, out_shape=jax.ShapeDtypeStruct((BANDS, CUT, 128),...  42.8 us
    unnamed x21, local copies, waits for them, and re-layouts  6.4 us

profile of v1, /device:TPU:100, one launch (start us, length us, event | category | flops | bytes accessed | tf_op | source)
XLA Modules:
  0.0 49.3 jit_solution(9367482161564552361)
XLA Ops:
  0.0 0.0 copy-start.8
  0.0 0.0 copy-start.9
  0.0 0.0 copy-start.6
  0.0 0.0 copy-start.7
  0.0 0.6 %copy-done.8 = s32[1,128]{1,0:T(1,128)S(1)} copy-done((s32[1,128]{1,0:T(1,128)S(1)}, s32[1,128]{1,0:T(1,128)}, u32[]{:S(2)}) %copy-start.8) | copy-done | bytes 536
  0.7 0.0 copy-done.9
  0.7 0.0 copy-done.6
  0.7 0.0 copy-done.7
  0.7 0.0 copy-start
  0.7 1.2 %copy-done = bf16[1,128,4096]{2,1,0:T(8,128)(2,1)S(1)} copy-done((bf16[1,128,4096]{2,1,0:T(8,128)(2,1)S(1)}, bf16[1,128,4096]{2,1,0:T(8,128)(2,1)}, u32[]{:S(2)}) %copy-start) | copy-done | bytes 1048600
  1.9 0.0 copy-start.1
  1.9 0.9 %copy-done.1 = f32[1,2,6,4096]{3,1,2,0:T(2,128)S(1)} copy-done((f32[1,2,6,4096]{3,1,2,0:T(2,128)S(1)}, f32[1,2,6,4096]{3,1,2,0:T(2,128)}, u32[]{:S(2)}) %copy-start.1) | copy-done | bytes 196632
  2.9 0.0 copy-start.2
  2.9 0.7 %copy-done.2 = bf16[1,4096]{1,0:T(2,128)(2,1)S(1)} copy-done((bf16[1,4096]{1,0:T(2,128)(2,1)S(1)}, bf16[1,4096]{1,0:T(2,128)(2,1)}, u32[]{:S(2)}) %copy-start.2) | copy-done | bytes 8216
  3.6 0.0 copy-start.3
  3.6 0.7 %copy-done.3 = bf16[1,4096]{1,0:T(2,128)(2,1)S(1)} copy-done((bf16[1,4096]{1,0:T(2,128)(2,1)S(1)}, bf16[1,4096]{1,0:T(2,128)(2,1)}, u32[]{:S(2)}) %copy-start.3) | copy-done | bytes 8216
  4.3 0.0 copy-start.4
  4.3 0.7 %copy-done.4 = bf16[1,4096]{1,0:T(2,128)(2,1)S(1)} copy-done((bf16[1,4096]{1,0:T(2,128)(2,1)S(1)}, bf16[1,4096]{1,0:T(2,128)(2,1)}, u32[]{:S(2)}) %copy-start.4) | copy-done | bytes 8216
  5.0 0.0 copy-start.5
  5.0 0.7 %copy-done.5 = bf16[1,4096]{1,0:T(2,128)(2,1)S(1)} copy-done((bf16[1,4096]{1,0:T(2,128)(2,1)S(1)}, bf16[1,4096]{1,0:T(2,128)(2,1)}, u32[]{:S(2)}) %copy-start.5) | copy-done | bytes 8216
  5.7 42.8 %shard_map.100 = f32[6,64,128]{2,1,0:T(8,128)S(1)} custom-call(f32[6,64,128]{2,1,0:T(8,128)S(1)} %bitcast.20, bf16[16,256,128]{2,1,0:T(8,128)(2,1)S(1)} %bitcast.18, f32[1,128]{1,0:T(1,128)S(1)} %copy-done.7, s32[1,128]{1,0:T(1,128)S(1)} %copy-done.8, s32[2,128]{1,0:T(2,128)S(1)} %bitcast.21, s32[1,2]{1,0:T(1,128)S(1)} %copy-done.9, ...), custom_call_target="tpu_custom_call" | custom-call | tf_op jit(solution)/shard_map/pallas_call | solution.py:352
  48.6 0.7 %copy.14 = f32[1,2,6,4096]{3,1,2,0:T(2,128)} copy(f32[1,2,6,4096]{3,1,2,0:T(2,128)S(1)} %bitcast.19) | data formatting | bytes 393216
Async XLA Ops:
  0.0 0.7 %copy-start.8 = (s32[1,128]{1,0:T(1,128)S(1)}, s32[1,128]{1,0:T(1,128)}, u32[]{:S(2)}) copy-start(s32[1,128]{1,0:T(1,128)} %coverage.1) | copy-start | bytes 1540
  0.0 0.7 %copy-start.9 = (s32[1,2]{1,0:T(1,128)S(1)}, s32[1,2]{1,0:T(1,128)}, u32[]{:S(2)}) copy-start(s32[1,2]{1,0:T(1,128)} %counts.1) | copy-start | bytes 28
  0.0 0.7 %copy-start.6 = (s32[1,128,2]{1,2,0:T(2,128)S(1)}, s32[1,128,2]{1,2,0:T(2,128)}, u32[]{:S(2)}) copy-start(s32[1,128,2]{1,2,0:T(2,128)} %param.14) | copy-start | bytes 3076
  0.0 0.7 %copy-start.7 = (f32[1,128]{1,0:T(1,128)S(1)}, f32[1,128]{1,0:T(1,128)}, u32[]{:S(2)}) copy-start(f32[1,128]{1,0:T(1,128)} %weights.1) | copy-start | bytes 1540
  0.7 1.2 %copy-start = (bf16[1,128,4096]{2,1,0:T(8,128)(2,1)S(1)}, bf16[1,128,4096]{2,1,0:T(8,128)(2,1)}, u32[]{:S(2)}) copy-start(bf16[1,128,4096]{2,1,0:T(8,128)(2,1)} %param.11) | copy-start | bytes 3145732
  1.9 0.9 %copy-start.1 = (f32[1,2,6,4096]{3,1,2,0:T(2,128)S(1)}, f32[1,2,6,4096]{3,1,2,0:T(2,128)}, u32[]{:S(2)}) copy-start(f32[1,2,6,4096]{3,1,2,0:T(2,128)} %param.10) | copy-start | bytes 589828
  2.9 0.7 %copy-start.2 = (bf16[1,4096]{1,0:T(2,128)(2,1)S(1)}, bf16[1,4096]{1,0:T(2,128)(2,1)}, u32[]{:S(2)}) copy-start(bf16[1,4096]{1,0:T(2,128)(2,1)} %psf_y.1) | copy-start | bytes 24580
  3.6 0.7 %copy-start.3 = (bf16[1,4096]{1,0:T(2,128)(2,1)S(1)}, bf16[1,4096]{1,0:T(2,128)(2,1)}, u32[]{:S(2)}) copy-start(bf16[1,4096]{1,0:T(2,128)(2,1)} %res_y.1) | copy-start | bytes 24580
  4.3 0.7 %copy-start.4 = (bf16[1,4096]{1,0:T(2,128)(2,1)S(1)}, bf16[1,4096]{1,0:T(2,128)(2,1)}, u32[]{:S(2)}) copy-start(bf16[1,4096]{1,0:T(2,128)(2,1)} %psf_x.1) | copy-start | bytes 24580
  5.0 0.7 %copy-start.5 = (bf16[1,4096]{1,0:T(2,128)(2,1)S(1)}, bf16[1,4096]{1,0:T(2,128)(2,1)}, u32[]{:S(2)}) copy-start(bf16[1,4096]{1,0:T(2,128)(2,1)} %res_x.1) | copy-start | bytes 24580

commit v2 on v1

--- a/solution.py
+++ b/solution.py
@@ -27,8 +27,8 @@
 
 
 def kernel(
-    models, obs_hbm, weights, coverage, offs, counts, psf_y, res_y, psf_x, res_x, out,
-    obs_v, obs_st, obs_in, models_low, mod_in, term_out, term_out2, term_in, term_in2,
+    models_h, obs_hbm, weights_h, coverage_h, offs_h, counts_h, psf_y_h, res_y_h, psf_x_h, res_x_h, out,
+    models, weights, coverage, offs, counts, psf_y, res_y, psf_x, res_x, obs_v, obs_st, obs_in, models_low, mod_in, term_out, term_out2, term_in, term_in2,
     mats, mats_in, tab_a, tab_at, tab_r, fold, rows_f, wide, spread,
     scale_v, scale_in, offs_in, off_own, off_par, sc_own, sc_par,
     in_s, in_r, in2_s, in2_r, obs_s, obs_r, t_s, t_r, t2_s, t2_r, small_s, small_r, local,
@@ -58,11 +58,21 @@
     for ky, kz in others:
         pl.semaphore_signal(barrier, inc=1, device_id={"epoch": device(*place(ky, kz))}, device_id_type=MESH)
 
+    mat_loads = [
+        pltpu.make_async_copy(src, dst, local.at[6 + i])
+        for i, (src, dst) in enumerate(((psf_y_h, psf_y), (res_y_h, res_y), (psf_x_h, psf_x), (res_x_h, res_x)))
+    ]
+    load_models = pltpu.make_async_copy(models_h, models, local.at[5])
     load_obs = pltpu.make_async_copy(obs_hbm, obs_v, local.at[0])
-    load_obs.start()
-    load_off = pltpu.make_async_copy(offs, off_own, local.at[1])
-    load_off.start()
-    scale_v[...] = weights[...] * coverage[...].astype(F32)
+    load_off = pltpu.make_async_copy(offs_h, off_own, local.at[1])
+    small_loads = [
+        pltpu.make_async_copy(src, dst, local.at[10 + i])
+        for i, (src, dst) in enumerate(
+            ((weights_h, weights), (coverage_h, coverage), (offs_h, offs), (counts_h, counts))
+        )
+    ]
+    for load in mat_loads + [load_models, load_obs, load_off] + small_loads:
+        load.start()
 
     straddle = jnp.int32(0)
     straddle_id = jnp.int32(0)
@@ -101,6 +111,8 @@
     def doubled(v):
         return jnp.where(low, v, pltpu.roll(v, CUT, 1))
 
+    for load in mat_loads:
+        load.wait()
     top, bottom = unfold(psf_y)
     first = jnp.concatenate([top, bottom], axis=0)[:, :CUT].astype(BF16)
     second = doubled(natural(res_y)).astype(BF16)
@@ -109,6 +121,7 @@
     second = doubled(natural(res_x)).astype(BF16)
     mats[1] = jnp.dot(first, second, preferred_element_type=F32).astype(BF16)
 
+    load_models.wait()
     for c in range(BANDS):
         models_low[c] = swap(models[c]).astype(BF16)
 
@@ -142,6 +155,9 @@
     lax.fori_loop(0, 16, relayout, 0)
 
     load_off.wait()
+    for load in small_loads:
+        load.wait()
+    scale_v[...] = weights[...] * coverage[...].astype(F32)
     load_scale = pltpu.make_async_copy(scale_v, sc_own, local.at[2])
     load_scale.start()
     load_scale.wait()
@@ -352,12 +368,18 @@
     updated = pl.pallas_call(
         kernel,
         out_shape=jax.ShapeDtypeStruct((BANDS, CUT, 128), F32),
-        in_specs=[
-            vmem, pl.BlockSpec(memory_space=pl.ANY), vmem, vmem, vmem, pl.BlockSpec(memory_space=pltpu.SMEM),
-            vmem, vmem, vmem, vmem,
-        ],
+        in_specs=[pl.BlockSpec(memory_space=pltpu.HBM)] * 10,
         out_specs=vmem,
         scratch_shapes=[
+            pltpu.VMEM((BANDS, CUT, 128), F32),
+            pltpu.VMEM((1, 128), F32),
+            pltpu.VMEM((1, 128), jnp.int32),
+            pltpu.VMEM((2, 128), jnp.int32),
+            pltpu.SMEM((1, 2), jnp.int32),
+            pltpu.VMEM((1, PIX2), BF16),
+            pltpu.VMEM((1, PIX2), BF16),
+            pltpu.VMEM((1, PIX2), BF16),
+            pltpu.VMEM((1, PIX2), BF16),
             pltpu.VMEM((16, 256, 128), BF16),
             pltpu.VMEM((2, NZ, NY, CUT, 128), BF16),
             pltpu.VMEM((NZ, NY, CUT, 128), BF16),
@@ -384,10 +406,10 @@
             pltpu.SMEM((1, 128), F32),
             pltpu.SMEM((1, 128), F32),
             dma((32,)), dma((32,)), dma((2,)), dma((32,)), dma((8,)), dma((8,)),
-            dma((32,)), dma((32,)), dma((32,)), dma((2,)), dma((3,)), dma((3,)), dma((5,)),
+            dma((32,)), dma((32,)), dma((32,)), dma((2,)), dma((3,)), dma((3,)), dma((14,)),
         ],
         compiler_params=pltpu.CompilerParams(
-            collective_id=0, has_side_effects=True, vmem_limit_bytes=48 * 2**20
+            collective_id=0, has_side_effects=True, vmem_limit_bytes=67043328
         ),
     )(
         pair_models, blocks, weights, coverage, offsets[0].T, counts, psf_y, resample_y, psf_x, resample_x

time: 49.7 us -> 45.2 us (0.909)
  local copies, waits for them, and re-layouts: 6.4 us -> 1.62 us
  Pallas kernels: 42.8 us -> 43.4 us
    unnamed x21 -> x1, local copies, waits for them, and re-layouts: 6.4 us -> 1.62 us
    pallas_call x1, Pallas kernels: 42.8 us -> 43.4 us  [on_device(): pl.pallas_call(kernel, out_shape=jax.ShapeDtypeStruct((BANDS, CUT, 128),...]
where the time goes in v2:
time: 45.2 us; the launch traced here: 45 us
  Pallas kernels  43.4 us (96%)
  local copies, waits for them, and re-layouts  1.62 us (4%)
    pallas_call x1, Pallas kernels, on_device(): pl.pallas_call(kernel, out_shape=jax.ShapeDtypeStruct((BANDS, CUT, 128),...  43.4 us
    unnamed x1, local copies, waits for them, and re-layouts  1.62 us

profile of v2, /device:TPU:100, one launch (start us, length us, event | category | flops | bytes accessed | tf_op | source)
XLA Modules:
  0.0 45.0 jit_solution(8935882174047344446)
XLA Ops:
  0.0 43.4 %shard_map.100 = f32[6,64,128]{2,1,0:T(8,128)} custom-call(f32[6,64,128]{2,1,0:T(8,128)} %bitcast.20, bf16[16,256,128]{2,1,0:T(8,128)(2,1)} %bitcast.18, f32[1,128]{1,0:T(1,128)} %weights_h.1, s32[1,128]{1,0:T(1,128)} %coverage_h.1, s32[2,128]{1,0:T(2,128)} %bitcast.21, s32[1,2]{1,0:T(1,128)} %counts_h.1, bf16[1,4096]{1,0:T(2,128)(2,1)} %psf_y_h.1, ...), custom_call_target="tpu_custom_call" | custom-call | tf_op jit(solution)/shard_map/pallas_call | solution.py:368
  43.4 1.6 %copy.14 = f32[1,2,6,4096]{3,1,2,0:T(2,128)} copy(f32[1,2,6,4096]{3,1,2,0:T(2,128)} %bitcast.19) | data formatting | bytes 393216

commit v3 on v2

--- a/solution.py
+++ b/solution.py
@@ -27,11 +27,11 @@
 
 
 def kernel(
-    models_h, obs_hbm, weights_h, coverage_h, offs_h, counts_h, psf_y_h, res_y_h, psf_x_h, res_x_h, out,
-    models, weights, coverage, offs, counts, psf_y, res_y, psf_x, res_x, obs_v, obs_st, obs_in, models_low, mod_in, term_out, term_out2, term_in, term_in2,
+    models_h, obs_hbm, weights_h, coverage_h, offs_h, counts_h, psf_y_h, res_y_h, psf_x_h, res_x_h, out_h,
+    out, models, weights, coverage, offs, counts, psf_y, res_y, psf_x, res_x, obs_v, obs_st, obs_in, models_low, mod_in, term_out, term_out2, term_in, term_in2,
     mats, mats_in, tab_a, tab_at, tab_r, fold, rows_f, wide, spread,
     scale_v, scale_in, offs_in, off_own, off_par, sc_own, sc_par,
-    in_s, in_r, in2_s, in2_r, obs_s, obs_r, t_s, t_r, t2_s, t2_r, small_s, small_r, local,
+    in_s, in_r, in2_s, in2_r, obs_s, obs_r, t_s, t_r, t2_s, t2_r, small_s, small_r, local, out_sem,
 ):
     me = lax.axis_index("epoch")
     x = lax.rem(me, 2)
@@ -111,6 +111,53 @@
     def doubled(v):
         return jnp.where(low, v, pltpu.roll(v, CUT, 1))
 
+    load_models.wait()
+    for c in range(BANDS):
+        models_low[c] = swap(models[c]).astype(BF16)
+
+    def tables(slot, source):
+        left = source[0].astype(F32)
+        right = source[1].astype(F32)
+        wide[...] = jnp.concatenate([left, left], axis=0).T
+
+        def one(d, carry):
+            tab_a[slot, d] = pltpu.roll(left, d, 1).astype(BF16)
+            tab_at[slot, d] = wide[pl.ds(CUT - d, CUT), :].astype(BF16)
+            tab_r[slot, d] = pltpu.roll(right, d, 1).astype(BF16)
+            return carry
+
+        lax.fori_loop(0, CUT, one, 0, unroll=4)
+
+    pl.semaphore_wait(barrier, 32)
+
+    def far_first(g):
+        return 4 + lax.div(g + 1, 2) * (1 - 2 * lax.rem(g, 2))
+
+    def model_copy(ky, kz):
+        yy, zz = place(ky, kz)
+        band = lax.div((yy * NZ + zz) * 2 * BANDS, E)
+        return remote(
+            models_low.at[band], mod_in.at[0, z * NY + y], in_s, in_r.at[z], device(yy, zz)
+        )
+
+    for ky, kz in others:
+        model_copy(ky, kz).start()
+    for i, (ys, zs) in enumerate(STRADDLERS):
+        band = band_of((ys * NZ + zs) * 2 + 1)
+        here = jnp.logical_and(y == ys, z == zs)
+
+        @pl.when(jnp.logical_not(here))
+        def _():
+            remote(
+                models_low.at[band], mod_in.at[1, z * NY + y], in2_s.at[i], in2_r.at[z], device(ys, zs)
+            ).start()
+
+        @pl.when(here)
+        def _():
+            mod_in[1, z * NY + y] = models_low[band]
+
+    mod_in[0, z * NY + y] = models_low[lax.div((y * NZ + z) * 2 * BANDS, E)]
+
     for load in mat_loads:
         load.wait()
     top, bottom = unfold(psf_y)
@@ -121,96 +168,51 @@
     second = doubled(natural(res_x)).astype(BF16)
     mats[1] = jnp.dot(first, second, preferred_element_type=F32).astype(BF16)
 
-    load_models.wait()
-    for c in range(BANDS):
-        models_low[c] = swap(models[c]).astype(BF16)
-
-    def tables(slot, source):
-        left = source[0].astype(F32)
-        right = source[1].astype(F32)
-        wide[...] = jnp.concatenate([left, left], axis=0).T
-
-        def one(d, carry):
-            tab_a[slot, d] = pltpu.roll(left, d, 1).astype(BF16)
-            tab_at[slot, d] = wide[pl.ds(CUT - d, CUT), :].astype(BF16)
-            tab_r[slot, d] = pltpu.roll(right, d, 1).astype(BF16)
-            return carry
-
-        lax.fori_loop(0, CUT, one, 0, unroll=4)
-
-    load_obs.wait()
-
-    def relayout(m, carry):
-        spread[...] = obs_v[m].astype(F32)
-        yy = lax.div(m, 4)
-        z2 = 2 * lax.rem(m, 4)
-        for s in range(4):
-            f0 = spread[pl.ds(2 * s, 32, stride=8), :]
-            f1 = spread[pl.ds(2 * s + 1, 32, stride=8), :]
-            top = jnp.where(low_half, f0, pltpu.roll(f1, CUT, 1))
-            bottom = jnp.where(low_half, pltpu.roll(f0, CUT, 1), f1)
-            obs_st[s % 2, z2 + s // 2, yy] = jnp.concatenate([top, bottom], axis=0).astype(BF16)
-        return carry
-
-    lax.fori_loop(0, 16, relayout, 0)
-
-    load_off.wait()
     for load in small_loads:
         load.wait()
     scale_v[...] = weights[...] * coverage[...].astype(F32)
-    load_scale = pltpu.make_async_copy(scale_v, sc_own, local.at[2])
-    load_scale.start()
-    load_scale.wait()
-
-    pl.semaphore_wait(barrier, 32)
-
     send_mats = remote(mats, mats_in, small_s.at[0], small_r.at[0], partner)
     send_off = remote(offs, offs_in, small_s.at[1], small_r.at[1], partner)
     send_scale = remote(scale_v, scale_in, small_s.at[2], small_r.at[2], partner)
     send_mats.start()
     send_off.start()
     send_scale.start()
+    load_scale = pltpu.make_async_copy(scale_v, sc_own, local.at[2])
+    load_scale.start()
+
+    load_obs.wait()
+
+    def relayout(z2):
+        def rows(yy, carry):
+            spread[...] = obs_v[yy * 4 + z2].astype(F32)
+            for s in range(4):
+                f0 = spread[pl.ds(2 * s, 32, stride=8), :]
+                f1 = spread[pl.ds(2 * s + 1, 32, stride=8), :]
+                top = jnp.where(low_half, f0, pltpu.roll(f1, CUT, 1))
+                bottom = jnp.where(low_half, pltpu.roll(f0, CUT, 1), f1)
+                obs_st[s % 2, 2 * z2 + s // 2, yy] = jnp.concatenate([top, bottom], axis=0).astype(BF16)
+            return carry
+
+        lax.fori_loop(0, NY, rows, 0)
 
     def obs_copy(g):
         zz = lax.rem(z + far_first(g), NZ)
-        return remote(obs_st.at[1 - x, zz], obs_in.at[zz], obs_s.at[g], obs_r.at[g], partner)
-
-    def far_first(g):
-        return 4 + lax.div(g + 1, 2) * (1 - 2 * lax.rem(g, 2))
-
-    for g in range(8):
-        obs_copy(jnp.int32(g)).start()
-
-    def model_copy(ky, kz):
-        yy, zz = place(ky, kz)
-        band = lax.div((yy * NZ + zz) * 2 * BANDS, E)
-        return remote(
-            models_low.at[band], mod_in.at[0, z, y], in_s.at[zz * NY + yy], in_r.at[z * NY + y], device(yy, zz)
-        )
-
-    for ky, kz in others:
-        model_copy(ky, kz).start()
-    for i, (ys, zs) in enumerate(STRADDLERS):
-        band = band_of((ys * NZ + zs) * 2 + 1)
-        here = jnp.logical_and(y == ys, z == zs)
-
-        @pl.when(jnp.logical_not(here))
-        def _():
-            remote(
-                models_low.at[band], mod_in.at[1, z, y], in2_s.at[i], in2_r.at[z * NY + y], device(ys, zs)
-            ).start()
-
-        @pl.when(here)
-        def _():
-            mod_in[1, z, y] = models_low[band]
-
-    mod_in[0, z, y] = models_low[lax.div((y * NZ + z) * 2 * BANDS, E)]
+        return remote(obs_st.at[1 - x, zz], obs_in.at[zz], obs_s, obs_r.at[g], partner)
+
+    farthest = lax.div(lax.rem(z + 4, NZ), 2)
+    for steps, groups in (((0,), (0,)), ((3, 1), (1, 2, 3, 4)), ((2,), (5, 6, 7))):
+        for step in steps:
+            relayout(lax.rem(farthest + step, 4))
+        for g in groups:
+            obs_copy(jnp.int32(g)).start()
 
     tables(0, mats)
     send_mats.wait_recv()
     tables(1, mats_in)
     send_off.wait_recv()
     send_scale.wait_recv()
+    load_off.wait()
+    load_scale.wait()
     load_off = pltpu.make_async_copy(offs_in, off_par, local.at[3])
     load_scale = pltpu.make_async_copy(scale_in, sc_par, local.at[4])
     load_off.start()
@@ -227,13 +229,16 @@
 
     def term_copy(yy, zz):
         return remote(
-            term_out.at[zz, yy], term_in.at[z, y], t_s.at[zz * NY + yy], t_r.at[z * NY + y], device(yy, zz)
+            term_out.at[zz * NY + yy], term_in.at[z * NY + y], t_s, t_r, device(yy, zz)
         )
 
     def term2_copy(yy, zz):
         return remote(
-            term_out2.at[zz, yy], term_in2.at[straddle_id], t2_s.at[zz * NY + yy], t2_r.at[straddle_id], device(yy, zz)
+            term_out2.at[zz * NY + yy], term_in2.at[straddle_id], t2_s, t2_r.at[straddle_id], device(yy, zz)
         )
+
+    def arrived(tiles, semaphore):
+        pltpu.make_async_copy(tiles, tiles, semaphore).wait()
 
     def split(v):
         return jnp.concatenate([v * mask_lo, v * mask_hi], axis=0)
@@ -241,22 +246,20 @@
     def group(g, carry):
         zz = lax.rem(z + far_first(g), NZ)
         obs_copy(g).wait_recv()
+
+        def arrive(count):
+            tiles = pl.ds(zz * NY, count)
+            arrived(mod_in.at[0, tiles], in_r.at[zz])
+
+            @pl.when(straddle == 1)
+            def _():
+                arrived(mod_in.at[1, tiles], in2_r.at[zz])
+
+        pl.when(g < 7)(lambda: arrive(NY))
+        pl.when(g == 7)(lambda: arrive(NY - 1))
         units = []
         for ky in (2, 1, 3, 0):
             yy = lax.rem(y + ky, NY)
-
-            def arrive():
-                slot = zz * NY + yy
-                remote(models_low.at[0], mod_in.at[0, zz, yy], in_s.at[slot], in_r.at[slot], partner).wait_recv()
-
-                @pl.when(straddle == 1)
-                def _():
-                    remote(models_low.at[0], mod_in.at[1, zz, yy], in_s.at[slot], in2_r.at[slot], partner).wait_recv()
-
-            if ky == 0:
-                pl.when(g < 7)(arrive)
-            else:
-                arrive()
             for e in range(2):
                 units.append((yy, e))
         state = []
@@ -265,7 +268,7 @@
             dy0, dx0 = offsets[e][0, b], offsets[e][1, b]
             dy1, dx1 = offsets[e][0, b + 1], offsets[e][1, b + 1]
             left = tab_a[e, dy0] * mask_lo + tab_a[e, dy1] * mask_hi
-            image = mod_in[slot_own if e == 0 else slot_par, zz, yy]
+            image = mod_in[slot_own if e == 0 else slot_par, zz * NY + yy]
             blurred = jnp.dot(left, split(image), preferred_element_type=F32).astype(BF16)
             state.append([yy, e, b, dy0, dy1, dx0, dx1, blurred])
         for s in state:
@@ -288,8 +291,8 @@
             )
         for yy, own, par in terms.values():
             zero = jnp.zeros_like(own)
-            term_out[zz, yy] = (jnp.where(own_first, own, zero) + jnp.where(par_first, par, zero)).astype(BF16)
-            term_out2[zz, yy] = (jnp.where(own_first, zero, own) + jnp.where(par_first, zero, par)).astype(BF16)
+            term_out[zz * NY + yy] = (jnp.where(own_first, own, zero) + jnp.where(par_first, par, zero)).astype(BF16)
+            term_out2[zz * NY + yy] = (jnp.where(own_first, zero, own) + jnp.where(par_first, zero, par)).astype(BF16)
         for ky in (2, 1, 3, 0):
             yy = lax.rem(y + ky, NY)
 
@@ -308,21 +311,29 @@
 
     lax.fori_loop(0, 8, group, 0)
 
-    term_in[z, y] = term_out[z, y]
+    term_in[z * NY + y] = term_out[z * NY + y]
 
     @pl.when(straddle == 1)
     def _():
-        term_in2[straddle_id] = term_out2[z, y]
-
-    for ky, kz in others:
-        yy, zz = place(ky, kz)
-        slot = zz * NY + yy
-        remote(term_out.at[zz, yy], term_in.at[zz, yy], t_s.at[slot], t_r.at[slot], partner).wait_recv()
+        term_in2[straddle_id] = term_out2[z * NY + y]
+
+    send_mats.wait_send()
+    send_off.wait_send()
+    send_scale.wait_send()
+    arrived(obs_in, obs_s)
+    arrived(mod_in.at[0, pl.ds(0, 31)], in_s)
     for i, (ys, zs) in enumerate(STRADDLERS):
 
         @pl.when(jnp.logical_not(jnp.logical_and(y == ys, z == zs)))
         def _():
-            remote(term_out2.at[0, 0], term_in2.at[i], t2_s.at[0], t2_r.at[i], partner).wait_recv()
+            arrived(models_low.at[0], in2_s.at[i])
+
+    arrived(term_in.at[pl.ds(0, 31)], t_r)
+    for i, (ys, zs) in enumerate(STRADDLERS):
+
+        @pl.when(jnp.logical_not(jnp.logical_and(y == ys, z == zs)))
+        def _():
+            arrived(term_in2.at[i], t2_r.at[i])
 
     seen_by = jnp.where(even, counts[0, 0].astype(F32), counts[0, 1].astype(F32))
     factor = step_size / seen_by
@@ -331,31 +342,20 @@
         for yy in range(NY):
             for zz in range(NZ):
                 if band_of((yy * NZ + zz) * 2) == c:
-                    total = total + term_in[zz, yy].astype(F32)
+                    total = total + term_in[zz * NY + yy].astype(F32)
         for i, (ys, zs) in enumerate(STRADDLERS):
             if band_of((ys * NZ + zs) * 2 + 1) == c:
                 total = total + term_in2[i].astype(F32)
-        out[c] = models[c] - factor * swap(total)
-
-    send_mats.wait_send()
-    send_off.wait_send()
-    send_scale.wait_send()
-    for g in range(8):
-        obs_copy(jnp.int32(g)).wait_send()
-    for ky, kz in others:
-        model_copy(ky, kz).wait_send()
-        yy, zz = place(ky, kz)
-        term_copy(yy, zz).wait_send()
-
-        @pl.when(straddle == 1)
-        def _():
-            term2_copy(yy, zz).wait_send()
-
-    for i, (ys, zs) in enumerate(STRADDLERS):
-
-        @pl.when(jnp.logical_not(jnp.logical_and(y == ys, z == zs)))
-        def _():
-            remote(models_low.at[0], mod_in.at[1, z, y], in2_s.at[i], in2_r.at[0], partner).wait_send()
+        out[c] = factor * swap(total)
+        pltpu.make_async_copy(out.at[c], out_h.at[c], out_sem).start()
+
+    arrived(term_out.at[pl.ds(0, 31)], t_s)
+
+    @pl.when(straddle == 1)
+    def _():
+        arrived(term_out2.at[pl.ds(0, 31)], t2_s)
+
+    arrived(out, out_sem)
 
 
 def on_device(
@@ -363,14 +363,14 @@
 ):
     pair_models = models[0].reshape(2, BANDS, 32, 128).transpose(1, 2, 0, 3).reshape(BANDS, CUT, 128)
     blocks = observed[0].reshape(16, 8, 32, 128).transpose(0, 2, 1, 3).reshape(16, 256, 128)
-    vmem = pl.BlockSpec(memory_space=pltpu.VMEM)
     dma = pltpu.SemaphoreType.DMA
-    updated = pl.pallas_call(
+    change = pl.pallas_call(
         kernel,
         out_shape=jax.ShapeDtypeStruct((BANDS, CUT, 128), F32),
         in_specs=[pl.BlockSpec(memory_space=pltpu.HBM)] * 10,
-        out_specs=vmem,
+        out_specs=pl.BlockSpec(memory_space=pl.ANY),
         scratch_shapes=[
+            pltpu.VMEM((BANDS, CUT, 128), F32),
             pltpu.VMEM((BANDS, CUT, 128), F32),
             pltpu.VMEM((1, 128), F32),
             pltpu.VMEM((1, 128), jnp.int32),
@@ -384,10 +384,10 @@
             pltpu.VMEM((2, NZ, NY, CUT, 128), BF16),
             pltpu.VMEM((NZ, NY, CUT, 128), BF16),
             pltpu.VMEM((BANDS, CUT, 128), BF16),
-            pltpu.VMEM((2, NZ, NY, CUT, 128), BF16),
-            pltpu.VMEM((NZ, NY, CUT, 128), BF16),
-            pltpu.VMEM((NZ, NY, CUT, 128), BF16),
-            pltpu.VMEM((NZ, NY, CUT, 128), BF16),
+            pltpu.VMEM((2, NZ * NY, CUT, 128), BF16),
+            pltpu.VMEM((NZ * NY, CUT, 128), BF16),
+            pltpu.VMEM((NZ * NY, CUT, 128), BF16),
+            pltpu.VMEM((NZ * NY, CUT, 128), BF16),
             pltpu.VMEM((len(STRADDLERS), CUT, 128), BF16),
             pltpu.VMEM((2, CUT, 128), BF16),
             pltpu.VMEM((2, CUT, 128), BF16),
@@ -405,15 +405,16 @@
             pltpu.SMEM((2, 128), jnp.int32),
             pltpu.SMEM((1, 128), F32),
             pltpu.SMEM((1, 128), F32),
-            dma((32,)), dma((32,)), dma((2,)), dma((32,)), dma((8,)), dma((8,)),
-            dma((32,)), dma((32,)), dma((32,)), dma((2,)), dma((3,)), dma((3,)), dma((14,)),
+            dma, dma((NZ,)), dma((2,)), dma((NZ,)), dma, dma((NZ,)),
+            dma, dma, dma, dma((2,)), dma((3,)), dma((3,)), dma((14,)), dma,
         ],
         compiler_params=pltpu.CompilerParams(
-            collective_id=0, has_side_effects=True, vmem_limit_bytes=67043328
+            collective_id=0, has_side_effects=True, vmem_limit_bytes=60_000_000
         ),
     )(
         pair_models, blocks, weights, coverage, offsets[0].T, counts, psf_y, resample_y, psf_x, resample_x
     )
+    updated = pair_models - change
     return updated.reshape(BANDS, 32, 2, 128).transpose(2, 0, 1, 3).reshape(1, 2, BANDS, PIX2)
 
 

time: 45.2 us -> 42 us (0.929)
  Pallas kernels: 43.4 us -> 40.2 us
  other arithmetic: 0 us -> 1.63 us
  local copies, waits for them, and re-layouts: 1.62 us -> 0.01 us
    pallas_call x1, Pallas kernels: 43.4 us -> 40.2 us  [on_device(): pl.pallas_call(kernel, out_shape=jax.ShapeDtypeStruct((BANDS, CUT, 128),...]
    sub x0 -> x1, other arithmetic: none -> 1.63 us  [on_device(): updated = pair_models - change]
    unnamed x1 -> x2, local copies, waits for them, and re-layouts: 1.62 us -> 0.01 us
where the time goes in v3:
time: 42 us; the launch traced here: 41.9 us
  Pallas kernels  40.2 us (96%)
  other arithmetic  1.63 us (4%)
    pallas_call x1, Pallas kernels, on_device(): pl.pallas_call(kernel, out_shape=jax.ShapeDtypeStruct((BANDS, CUT, 128),...  40.2 us
    sub x1, other arithmetic, on_device(): updated = pair_models - change  1.63 us

profile of v3, /device:TPU:100, one launch (start us, length us, event | category | flops | bytes accessed | tf_op | source)
XLA Modules:
  0.0 41.9 jit_solution(5357398450869687676)
XLA Ops:
  0.0 0.0 copy-start
  0.0 40.2 %shard_map.100 = f32[6,64,128]{2,1,0:T(8,128)} custom-call(f32[6,64,128]{2,1,0:T(8,128)} %bitcast.19, bf16[16,256,128]{2,1,0:T(8,128)(2,1)} %bitcast.18, f32[1,128]{1,0:T(1,128)} %weights_h.1, s32[1,128]{1,0:T(1,128)} %coverage_h.1, s32[2,128]{1,0:T(2,128)} %bitcast.21, s32[1,2]{1,0:T(1,128)} %counts_h.1, bf16[1,4096]{1,0:T(2,128)(2,1)} %psf_y_h.1, ...), custom_call_target="tpu_custom_call" | custom-call | tf_op jit(solution)/shard_map/pallas_call | solution.py:367
  40.2 0.0 copy-done
  40.2 1.6 %sub.3 = f32[6,64,128]{2,1,0:T(8,128)} subtract(f32[6,64,128]{2,1,0:T(8,128)S(1)} %bitcast.20, f32[6,64,128]{2,1,0:T(8,128)} %shard_map.100) | non-fusion elementwise | flops 49152 | bytes 589824 | tf_op jit(solution)/shard_map/sub | solution.py:417
Async XLA Ops:
  0.0 40.2 %copy-start = (f32[1,2,6,4096]{3,1,2,0:T(2,128)S(1)}, f32[1,2,6,4096]{3,1,2,0:T(2,128)}, u32[]{:S(2)}) copy-start(f32[1,2,6,4096]{3,1,2,0:T(2,128)} %param.10) | copy-start | bytes 589828

commit v4 on v3

--- a/solution.py
+++ b/solution.py
@@ -45,7 +45,7 @@
     def place(ky, kz):
         return lax.rem(y + ky, NY), lax.rem(z + kz, NZ)
 
-    relative = [(ky, kz) for kz in (4, 3, 5, 2, 6, 1, 7, 0) for ky in (2, 1, 3, 0)]
+    relative = [(ky, kz) for kz in (4, 3, 5, 2, 6, 1, 7, 0) for ky in (2, 3, 1, 0)]
     others = [r for r in relative if r != (0, 0)]
 
     def remote(src, dst, send, recv, target):
@@ -71,7 +71,8 @@
             ((weights_h, weights), (coverage_h, coverage), (offs_h, offs), (counts_h, counts))
         )
     ]
-    for load in mat_loads + [load_models, load_obs, load_off] + small_loads:
+    load_models.start()
+    for load in mat_loads + [load_off] + small_loads:
         load.start()
 
     straddle = jnp.int32(0)
@@ -112,6 +113,7 @@
         return jnp.where(low, v, pltpu.roll(v, CUT, 1))
 
     load_models.wait()
+    load_obs.start()
     for c in range(BANDS):
         models_low[c] = swap(models[c]).astype(BF16)
 
@@ -140,8 +142,6 @@
             models_low.at[band], mod_in.at[0, z * NY + y], in_s, in_r.at[z], device(yy, zz)
         )
 
-    for ky, kz in others:
-        model_copy(ky, kz).start()
     for i, (ys, zs) in enumerate(STRADDLERS):
         band = band_of((ys * NZ + zs) * 2 + 1)
         here = jnp.logical_and(y == ys, z == zs)
@@ -155,6 +155,9 @@
         @pl.when(here)
         def _():
             mod_in[1, z * NY + y] = models_low[band]
+
+    for ky, kz in others:
+        model_copy(ky, kz).start()
 
     mod_in[0, z * NY + y] = models_low[lax.div((y * NZ + z) * 2 * BANDS, E)]
 
@@ -258,7 +261,7 @@
         pl.when(g < 7)(lambda: arrive(NY))
         pl.when(g == 7)(lambda: arrive(NY - 1))
         units = []
-        for ky in (2, 1, 3, 0):
+        for ky in (2, 3, 1, 0):
             yy = lax.rem(y + ky, NY)
             for e in range(2):
                 units.append((yy, e))
@@ -293,7 +296,7 @@
             zero = jnp.zeros_like(own)
             term_out[zz * NY + yy] = (jnp.where(own_first, own, zero) + jnp.where(par_first, par, zero)).astype(BF16)
             term_out2[zz * NY + yy] = (jnp.where(own_first, zero, own) + jnp.where(par_first, zero, par)).astype(BF16)
-        for ky in (2, 1, 3, 0):
+        for ky in (2, 3, 1, 0):
             yy = lax.rem(y + ky, NY)
 
             def ship():

time: 42 us -> 39 us (0.929); the launches traced: 41.9 us -> 38.4 us
  Pallas kernels: 40.2 us -> 36.8 us
    pallas_call x1, Pallas kernels: 40.2 us -> 36.8 us  [on_device(): pl.pallas_call(kernel, out_shape=jax.ShapeDtypeStruct((BANDS, CUT, 128),...]
where the time goes in v4:
time: 39 us; the launch traced here: 38.4 us
  Pallas kernels  36.8 us (94%)
  other arithmetic  1.63 us (4%)
    pallas_call x1, Pallas kernels, on_device(): pl.pallas_call(kernel, out_shape=jax.ShapeDtypeStruct((BANDS, CUT, 128),...  36.8 us
    sub x1, other arithmetic, on_device(): updated = pair_models - change  1.63 us

profile of v4, /device:TPU:100, one launch (start us, length us, event | category | flops | bytes accessed | tf_op | source)
XLA Modules:
  0.0 38.4 jit_solution(15090608817823925096)
XLA Ops:
  0.0 0.0 copy-start
  0.0 36.8 %shard_map.100 = f32[6,64,128]{2,1,0:T(8,128)} custom-call(f32[6,64,128]{2,1,0:T(8,128)} %bitcast.19, bf16[16,256,128]{2,1,0:T(8,128)(2,1)} %bitcast.18, f32[1,128]{1,0:T(1,128)} %weights_h.1, s32[1,128]{1,0:T(1,128)} %coverage_h.1, s32[2,128]{1,0:T(2,128)} %bitcast.21, s32[1,2]{1,0:T(1,128)} %counts_h.1, bf16[1,4096]{1,0:T(2,128)(2,1)} %psf_y_h.1, ...), custom_call_target="tpu_custom_call" | custom-call | tf_op jit(solution)/shard_map/pallas_call | solution.py:370
  36.8 0.0 copy-done
  36.8 1.6 %sub.3 = f32[6,64,128]{2,1,0:T(8,128)} subtract(f32[6,64,128]{2,1,0:T(8,128)S(1)} %bitcast.20, f32[6,64,128]{2,1,0:T(8,128)} %shard_map.100) | non-fusion elementwise | flops 49152 | bytes 589824 | tf_op jit(solution)/shard_map/sub | solution.py:420
Async XLA Ops:
  0.0 36.8 %copy-start = (f32[1,2,6,4096]{3,1,2,0:T(2,128)S(1)}, f32[1,2,6,4096]{3,1,2,0:T(2,128)}, u32[]{:S(2)}) copy-start(f32[1,2,6,4096]{3,1,2,0:T(2,128)} %param.10) | copy-start | bytes 589828

commit v5 on v4

--- a/solution.py
+++ b/solution.py
@@ -12,6 +12,8 @@
 PIX2 = 4096
 E = 64
 NY, NZ = 4, 8
+KY = (2, 3, 1, 0)
+ORDER = (5, 3, 4, 6, 2, 7, 1, 0)
 step_size = 0.5
 MESH = pl.DeviceIdType.MESH
 F32, BF16 = jnp.float32, jnp.bfloat16
@@ -45,7 +47,7 @@
     def place(ky, kz):
         return lax.rem(y + ky, NY), lax.rem(z + kz, NZ)
 
-    relative = [(ky, kz) for kz in (4, 3, 5, 2, 6, 1, 7, 0) for ky in (2, 3, 1, 0)]
+    relative = [(ky, kz) for kz in ORDER for ky in KY]
     others = [r for r in relative if r != (0, 0)]
 
     def remote(src, dst, send, recv, target):
@@ -132,8 +134,11 @@
 
     pl.semaphore_wait(barrier, 32)
 
-    def far_first(g):
-        return 4 + lax.div(g + 1, 2) * (1 - 2 * lax.rem(g, 2))
+    def turn(g):
+        kz = jnp.int32(ORDER[0])
+        for i in range(1, NZ):
+            kz = jnp.where(g == i, ORDER[i], kz)
+        return kz
 
     def model_copy(ky, kz):
         yy, zz = place(ky, kz)
@@ -199,15 +204,13 @@
         lax.fori_loop(0, NY, rows, 0)
 
     def obs_copy(g):
-        zz = lax.rem(z + far_first(g), NZ)
+        zz = lax.rem(z + turn(g), NZ)
         return remote(obs_st.at[1 - x, zz], obs_in.at[zz], obs_s, obs_r.at[g], partner)
 
-    farthest = lax.div(lax.rem(z + 4, NZ), 2)
-    for steps, groups in (((0,), (0,)), ((3, 1), (1, 2, 3, 4)), ((2,), (5, 6, 7))):
-        for step in steps:
-            relayout(lax.rem(farthest + step, 4))
-        for g in groups:
-            obs_copy(jnp.int32(g)).start()
+    for z2 in range(4):
+        relayout(z2)
+    for g in range(NZ):
+        obs_copy(jnp.int32(g)).start()
 
     tables(0, mats)
     send_mats.wait_recv()
@@ -247,7 +250,9 @@
         return jnp.concatenate([v * mask_lo, v * mask_hi], axis=0)
 
     def group(g, carry):
-        zz = lax.rem(z + far_first(g), NZ)
+        kz = turn(g)
+        home = kz == 0
+        zz = lax.rem(z + kz, NZ)
         obs_copy(g).wait_recv()
 
         def arrive(count):
@@ -258,10 +263,10 @@
             def _():
                 arrived(mod_in.at[1, tiles], in2_r.at[zz])
 
-        pl.when(g < 7)(lambda: arrive(NY))
-        pl.when(g == 7)(lambda: arrive(NY - 1))
+        pl.when(jnp.logical_not(home))(lambda: arrive(NY))
+        pl.when(home)(lambda: arrive(NY - 1))
         units = []
-        for ky in (2, 3, 1, 0):
+        for ky in KY:
             yy = lax.rem(y + ky, NY)
             for e in range(2):
                 units.append((yy, e))
@@ -296,7 +301,7 @@
             zero = jnp.zeros_like(own)
             term_out[zz * NY + yy] = (jnp.where(own_first, own, zero) + jnp.where(par_first, par, zero)).astype(BF16)
             term_out2[zz * NY + yy] = (jnp.where(own_first, zero, own) + jnp.where(par_first, zero, par)).astype(BF16)
-        for ky in (2, 3, 1, 0):
+        for ky in KY:
             yy = lax.rem(y + ky, NY)
 
             def ship():
@@ -307,7 +312,7 @@
                     term2_copy(yy, zz).start()
 
             if ky == 0:
-                pl.when(g < 7)(ship)
+                pl.when(jnp.logical_not(home))(ship)
             else:
                 ship()
         return carry

time: 39 us -> 38.5 us (0.987); the launches traced: 38.4 us -> 38.4 us
  no operation moved by 1% of the time
where the time goes in v5:
time: 38.5 us; the launch traced here: 38.4 us
  Pallas kernels  36.7 us (95%)
  other arithmetic  1.63 us (4%)
    pallas_call x1, Pallas kernels, on_device(): pl.pallas_call(kernel, out_shape=jax.ShapeDtypeStruct((BANDS, CUT, 128),...  36.7 us
    sub x1, other arithmetic, on_device(): updated = pair_models - change  1.63 us

profile of v5, /device:TPU:100, one launch (start us, length us, event | category | flops | bytes accessed | tf_op | source)
XLA Modules:
  0.0 38.4 jit_solution(13652051139573566313)
XLA Ops:
  0.0 0.0 copy-start
  0.0 36.7 %shard_map.100 = f32[6,64,128]{2,1,0:T(8,128)} custom-call(f32[6,64,128]{2,1,0:T(8,128)} %bitcast.19, bf16[16,256,128]{2,1,0:T(8,128)(2,1)} %bitcast.18, f32[1,128]{1,0:T(1,128)} %weights_h.1, s32[1,128]{1,0:T(1,128)} %coverage_h.1, s32[2,128]{1,0:T(2,128)} %bitcast.21, s32[1,2]{1,0:T(1,128)} %counts_h.1, bf16[1,4096]{1,0:T(2,128)(2,1)} %psf_y_h.1, ...), custom_call_target="tpu_custom_call" | custom-call | tf_op jit(solution)/shard_map/pallas_call | solution.py:375
  36.7 0.0 copy-done
  36.7 1.6 %sub.3 = f32[6,64,128]{2,1,0:T(8,128)} subtract(f32[6,64,128]{2,1,0:T(8,128)S(1)} %bitcast.20, f32[6,64,128]{2,1,0:T(8,128)} %shard_map.100) | non-fusion elementwise | flops 49152 | bytes 589824 | tf_op jit(solution)/shard_map/sub | solution.py:425
Async XLA Ops:
  0.0 36.7 %copy-start = (f32[1,2,6,4096]{3,1,2,0:T(2,128)S(1)}, f32[1,2,6,4096]{3,1,2,0:T(2,128)}, u32[]{:S(2)}) copy-start(f32[1,2,6,4096]{3,1,2,0:T(2,128)} %param.10) | copy-start | bytes 589828

commit v6 on v5

--- a/solution.py
+++ b/solution.py
@@ -28,12 +28,49 @@
 ]
 
 
+def swap(v):
+    low = lax.broadcasted_iota(jnp.int32, (CUT, 128), 1) < CUT
+    even = lax.rem(lax.broadcasted_iota(jnp.int32, (CUT, 128), 0), 2) == 0
+    turned = pltpu.roll(v, CUT, 1)
+    up = pltpu.roll(turned, CUT - 1, 0)
+    down = pltpu.roll(turned, 1, 0)
+    return jnp.where(low, jnp.where(even, v, down), jnp.where(even, up, v))
+
+
+def finish(models_h, terms_h, terms2_h, counts_h, updated_h, models, terms, terms2, counts, updated, sems):
+    loads = [
+        pltpu.make_async_copy(src, dst, sems.at[i])
+        for i, (src, dst) in enumerate(
+            ((counts_h, counts), (terms2_h, terms2), (terms_h, terms), (models_h, models))
+        )
+    ]
+    for load in loads:
+        load.start()
+    for load in loads:
+        load.wait()
+    even = lax.rem(lax.broadcasted_iota(jnp.int32, (CUT, 128), 0), 2) == 0
+    seen_by = jnp.where(even, counts[0, 0].astype(F32), counts[0, 1].astype(F32))
+    factor = step_size / seen_by
+    for c in range(BANDS):
+        total = jnp.zeros((CUT, 128), F32)
+        for yy in range(NY):
+            for zz in range(NZ):
+                if band_of((yy * NZ + zz) * 2) == c:
+                    total = total + terms[zz * NY + yy].astype(F32)
+        for i, (ys, zs) in enumerate(STRADDLERS):
+            if band_of((ys * NZ + zs) * 2 + 1) == c:
+                total = total + terms2[i].astype(F32)
+        updated[c] = models[c] - factor * swap(total)
+        pltpu.make_async_copy(updated.at[c], updated_h.at[c], sems.at[4]).start()
+    pltpu.make_async_copy(updated, updated_h, sems.at[4]).wait()
+
+
 def kernel(
-    models_h, obs_hbm, weights_h, coverage_h, offs_h, counts_h, psf_y_h, res_y_h, psf_x_h, res_x_h, out_h,
-    out, models, weights, coverage, offs, counts, psf_y, res_y, psf_x, res_x, obs_v, obs_st, obs_in, models_low, mod_in, term_out, term_out2, term_in, term_in2,
+    models_h, obs_hbm, weights_h, coverage_h, offs_h, psf_y_h, res_y_h, psf_x_h, res_x_h, term_in, term_in2,
+    models, weights, coverage, offs, psf_y, res_y, psf_x, res_x, obs_v, obs_st, obs_in, models_low, mod_in, term_out, term_out2,
     mats, mats_in, tab_a, tab_at, tab_r, fold, rows_f, wide, spread,
     scale_v, scale_in, offs_in, off_own, off_par, sc_own, sc_par,
-    in_s, in_r, in2_s, in2_r, obs_s, obs_r, t_s, t_r, t2_s, t2_r, small_s, small_r, local, out_sem,
+    in_s, in_r, in2_s, in2_r, obs_s, obs_r, t_s, t_r, t2_s, t2_r, small_s, small_r, local, home_sem,
 ):
     me = lax.axis_index("epoch")
     x = lax.rem(me, 2)
@@ -70,7 +107,7 @@
     small_loads = [
         pltpu.make_async_copy(src, dst, local.at[10 + i])
         for i, (src, dst) in enumerate(
-            ((weights_h, weights), (coverage_h, coverage), (offs_h, offs), (counts_h, counts))
+            ((weights_h, weights), (coverage_h, coverage), (offs_h, offs))
         )
     ]
     load_models.start()
@@ -91,12 +128,6 @@
     even = lax.rem(row, 2) == 0
     mask_lo = jnp.where(low, 1.0, 0.0).astype(BF16)
     mask_hi = jnp.where(low, 0.0, 1.0).astype(BF16)
-
-    def swap(v):
-        turned = pltpu.roll(v, CUT, 1)
-        up = pltpu.roll(turned, CUT - 1, 0)
-        down = pltpu.roll(turned, 1, 0)
-        return jnp.where(low, jnp.where(even, v, down), jnp.where(even, up, v))
 
     def unfold(ref):
         v = ref[...].astype(F32)
@@ -319,11 +350,12 @@
 
     lax.fori_loop(0, 8, group, 0)
 
-    term_in[z * NY + y] = term_out[z * NY + y]
+    home = z * NY + y
+    pltpu.make_async_copy(term_out.at[home], term_in.at[home], home_sem.at[0]).start()
 
     @pl.when(straddle == 1)
     def _():
-        term_in2[straddle_id] = term_out2[z * NY + y]
+        pltpu.make_async_copy(term_out2.at[home], term_in2.at[straddle_id], home_sem.at[1]).start()
 
     send_mats.wait_send()
     send_off.wait_send()
@@ -343,27 +375,13 @@
         def _():
             arrived(term_in2.at[i], t2_r.at[i])
 
-    seen_by = jnp.where(even, counts[0, 0].astype(F32), counts[0, 1].astype(F32))
-    factor = step_size / seen_by
-    for c in range(BANDS):
-        total = jnp.zeros((CUT, 128), F32)
-        for yy in range(NY):
-            for zz in range(NZ):
-                if band_of((yy * NZ + zz) * 2) == c:
-                    total = total + term_in[zz * NY + yy].astype(F32)
-        for i, (ys, zs) in enumerate(STRADDLERS):
-            if band_of((ys * NZ + zs) * 2 + 1) == c:
-                total = total + term_in2[i].astype(F32)
-        out[c] = factor * swap(total)
-        pltpu.make_async_copy(out.at[c], out_h.at[c], out_sem).start()
-
+    arrived(term_in.at[0], home_sem.at[0])
     arrived(term_out.at[pl.ds(0, 31)], t_s)
 
     @pl.when(straddle == 1)
     def _():
         arrived(term_out2.at[pl.ds(0, 31)], t2_s)
-
-    arrived(out, out_sem)
+        arrived(term_in2.at[0], home_sem.at[1])
 
 
 def on_device(
@@ -371,19 +389,21 @@
 ):
     pair_models = models[0].reshape(2, BANDS, 32, 128).transpose(1, 2, 0, 3).reshape(BANDS, CUT, 128)
     blocks = observed[0].reshape(16, 8, 32, 128).transpose(0, 2, 1, 3).reshape(16, 256, 128)
+    anywhere = pl.BlockSpec(memory_space=pl.ANY)
     dma = pltpu.SemaphoreType.DMA
-    change = pl.pallas_call(
+    terms, terms2 = pl.pallas_call(
         kernel,
-        out_shape=jax.ShapeDtypeStruct((BANDS, CUT, 128), F32),
-        in_specs=[pl.BlockSpec(memory_space=pltpu.HBM)] * 10,
-        out_specs=pl.BlockSpec(memory_space=pl.ANY),
+        out_shape=(
+            jax.ShapeDtypeStruct((NZ * NY, CUT, 128), BF16),
+            jax.ShapeDtypeStruct((len(STRADDLERS), CUT, 128), BF16),
+        ),
+        in_specs=[anywhere] * 9,
+        out_specs=(anywhere, anywhere),
         scratch_shapes=[
-            pltpu.VMEM((BANDS, CUT, 128), F32),
             pltpu.VMEM((BANDS, CUT, 128), F32),
             pltpu.VMEM((1, 128), F32),
             pltpu.VMEM((1, 128), jnp.int32),
             pltpu.VMEM((2, 128), jnp.int32),
-            pltpu.SMEM((1, 2), jnp.int32),
             pltpu.VMEM((1, PIX2), BF16),
             pltpu.VMEM((1, PIX2), BF16),
             pltpu.VMEM((1, PIX2), BF16),
@@ -395,8 +415,6 @@
             pltpu.VMEM((2, NZ * NY, CUT, 128), BF16),
             pltpu.VMEM((NZ * NY, CUT, 128), BF16),
             pltpu.VMEM((NZ * NY, CUT, 128), BF16),
-            pltpu.VMEM((NZ * NY, CUT, 128), BF16),
-            pltpu.VMEM((len(STRADDLERS), CUT, 128), BF16),
             pltpu.VMEM((2, CUT, 128), BF16),
             pltpu.VMEM((2, CUT, 128), BF16),
             pltpu.VMEM((2, CUT, CUT, 128), BF16),
@@ -414,15 +432,29 @@
             pltpu.SMEM((1, 128), F32),
             pltpu.SMEM((1, 128), F32),
             dma, dma((NZ,)), dma((2,)), dma((NZ,)), dma, dma((NZ,)),
-            dma, dma, dma, dma((2,)), dma((3,)), dma((3,)), dma((14,)), dma,
+            dma, dma, dma, dma((2,)), dma((3,)), dma((3,)), dma((13,)), dma((2,)),
         ],
         compiler_params=pltpu.CompilerParams(
             collective_id=0, has_side_effects=True, vmem_limit_bytes=60_000_000
         ),
     )(
-        pair_models, blocks, weights, coverage, offsets[0].T, counts, psf_y, resample_y, psf_x, resample_x
+        pair_models, blocks, weights, coverage, offsets[0].T, psf_y, resample_y, psf_x, resample_x
     )
-    updated = pair_models - change
+    updated = pl.pallas_call(
+        finish,
+        out_shape=jax.ShapeDtypeStruct((BANDS, CUT, 128), F32),
+        in_specs=[anywhere] * 4,
+        out_specs=anywhere,
+        scratch_shapes=[
+            pltpu.VMEM((BANDS, CUT, 128), F32),
+            pltpu.VMEM((NZ * NY, CUT, 128), BF16),
+            pltpu.VMEM((len(STRADDLERS), CUT, 128), BF16),
+            pltpu.SMEM((1, 2), jnp.int32),
+            pltpu.VMEM((BANDS, CUT, 128), F32),
+            dma((5,)),
+        ],
+        compiler_params=pltpu.CompilerParams(vmem_limit_bytes=60_000_000),
+    )(pair_models, terms, terms2, counts)
     return updated.reshape(BANDS, 32, 2, 128).transpose(2, 0, 1, 3).reshape(1, 2, BANDS, PIX2)
 
 

time: 38.5 us -> 38.1 us (0.990)
  other arithmetic: 1.63 us -> 0 us
  Pallas kernels: 36.7 us -> 38 us
    sub x1 -> x0, other arithmetic: 1.63 us -> none  [on_device(): updated = pair_models - change]
    pallas_call x1 -> x2, Pallas kernels: 36.7 us -> 38 us  [the longest x1 36.1 us: on_device(): pl.pallas_call(kernel, out_shape=(jax.ShapeDtypeStruct((NZ * NY, CUT, 128...]
where the time goes in v6:
time: 38.1 us; the launch traced here: 38 us
  Pallas kernels  38 us (100%)
    pallas_call x1, Pallas kernels, on_device(): pl.pallas_call(kernel, out_shape=(jax.ShapeDtypeStruct((NZ * NY, CUT, 128...  36.1 us
    pallas_call x1, Pallas kernels, on_device(): pl.pallas_call(finish, out_shape=jax.ShapeDtypeStruct((BANDS, CUT, 128),...  1.91 us

profile of v6, /device:TPU:100, one launch (start us, length us, event | category | flops | bytes accessed | tf_op | source)
XLA Modules:
  0.0 38.0 jit_solution(9716433597083074534)
XLA Ops:
  0.0 36.1 %shard_map.100 = (bf16[32,64,128]{2,1,0:T(8,128)(2,1)}, bf16[2,64,128]{2,1,0:T(8,128)(2,1)}) custom-call(f32[6,64,128]{2,1,0:T(8,128)} %bitcast.19, bf16[16,256,128]{2,1,0:T(8,128)(2,1)} %bitcast.18, f32[1,128]{1,0:T(1,128)} %weights_h.1, s32[1,128]{1,0:T(1,128)} %coverage_h.1, s32[2,128]{1,0:T(2,128)} %bitcast.21, bf16[1,4096]{1,0:T(2,128)(2,1)} %psf_y_h.1, ...), custom_call_target="tpu_custom_call" | custom-call | tf_op jit(solution)/shard_map/pallas_call | solution.py:394
  36.1 1.9 %shard_map.101 = f32[6,64,128]{2,1,0:T(8,128)} custom-call(f32[6,64,128]{2,1,0:T(8,128)} %bitcast.20, bf16[32,64,128]{2,1,0:T(8,128)(2,1)} %get-tuple-element.7.terms_h, bf16[2,64,128]{2,1,0:T(8,128)(2,1)} %get-tuple-element.8.terms2_h, s32[1,2]{1,0:T(1,128)} %counts_h.1), custom_call_target="tpu_custom_call" | custom-call | tf_op jit(solution)/shard_map/pallas_call | solution.py:443

commit v7 on v6

--- a/solution.py
+++ b/solution.py
@@ -41,7 +41,13 @@
     loads = [
         pltpu.make_async_copy(src, dst, sems.at[i])
         for i, (src, dst) in enumerate(
-            ((counts_h, counts), (terms2_h, terms2), (terms_h, terms), (models_h, models))
+            (
+                (terms_h.at[pl.ds(0, 16)], terms.at[pl.ds(0, 16)]),
+                (terms_h.at[pl.ds(16, 16)], terms.at[pl.ds(16, 16)]),
+                (terms2_h, terms2),
+                (models_h, models),
+                (counts_h, counts),
+            )
         )
     ]
     for load in loads:
@@ -61,8 +67,8 @@
             if band_of((ys * NZ + zs) * 2 + 1) == c:
                 total = total + terms2[i].astype(F32)
         updated[c] = models[c] - factor * swap(total)
-        pltpu.make_async_copy(updated.at[c], updated_h.at[c], sems.at[4]).start()
-    pltpu.make_async_copy(updated, updated_h, sems.at[4]).wait()
+        pltpu.make_async_copy(updated.at[c], updated_h.at[c], sems.at[5]).start()
+    pltpu.make_async_copy(updated, updated_h, sems.at[5]).wait()
 
 
 def kernel(
@@ -70,7 +76,7 @@
     models, weights, coverage, offs, psf_y, res_y, psf_x, res_x, obs_v, obs_st, obs_in, models_low, mod_in, term_out, term_out2,
     mats, mats_in, tab_a, tab_at, tab_r, fold, rows_f, wide, spread,
     scale_v, scale_in, offs_in, off_own, off_par, sc_own, sc_par,
-    in_s, in_r, in2_s, in2_r, obs_s, obs_r, t_s, t_r, t2_s, t2_r, small_s, small_r, local, home_sem,
+    in_s, in_r, in2_s, obs_s, obs_r, t_s, t_r, t2_s, t2_r, small_s, small_r, local, home_sem,
 ):
     me = lax.axis_index("epoch")
     x = lax.rem(me, 2)
@@ -185,7 +191,7 @@
         @pl.when(jnp.logical_not(here))
         def _():
             remote(
-                models_low.at[band], mod_in.at[1, z * NY + y], in2_s.at[i], in2_r.at[z], device(ys, zs)
+                models_low.at[band], mod_in.at[1, z * NY + y], in2_s.at[i], in_r.at[z], device(ys, zs)
             ).start()
 
         @pl.when(here)
@@ -288,11 +294,8 @@
 
         def arrive(count):
             tiles = pl.ds(zz * NY, count)
-            arrived(mod_in.at[0, tiles], in_r.at[zz])
-
-            @pl.when(straddle == 1)
-            def _():
-                arrived(mod_in.at[1, tiles], in2_r.at[zz])
+            pl.when(straddle == 0)(lambda: arrived(mod_in.at[0, tiles], in_r.at[zz]))
+            pl.when(straddle == 1)(lambda: arrived(mod_in.at[:, tiles], in_r.at[zz]))
 
         pl.when(jnp.logical_not(home))(lambda: arrive(NY))
         pl.when(home)(lambda: arrive(NY - 1))
@@ -431,7 +434,7 @@
             pltpu.SMEM((2, 128), jnp.int32),
             pltpu.SMEM((1, 128), F32),
             pltpu.SMEM((1, 128), F32),
-            dma, dma((NZ,)), dma((2,)), dma((NZ,)), dma, dma((NZ,)),
+            dma, dma((NZ,)), dma((2,)), dma, dma((NZ,)),
             dma, dma, dma, dma((2,)), dma((3,)), dma((3,)), dma((13,)), dma((2,)),
         ],
         compiler_params=pltpu.CompilerParams(
@@ -451,7 +454,7 @@
             pltpu.VMEM((len(STRADDLERS), CUT, 128), BF16),
             pltpu.SMEM((1, 2), jnp.int32),
             pltpu.VMEM((BANDS, CUT, 128), F32),
-            dma((5,)),
+            dma((6,)),
         ],
         compiler_params=pltpu.CompilerParams(vmem_limit_bytes=60_000_000),
     )(pair_models, terms, terms2, counts)

time: 38.1 us -> 38.1 us (level)
  no operation moved by 1% of the time
where the time goes in v7:
time: 38.1 us; the launch traced here: 37.9 us
  Pallas kernels  37.9 us (99%)
    pallas_call x1, Pallas kernels, on_device(): pl.pallas_call(kernel, out_shape=(jax.ShapeDtypeStruct((NZ * NY, CUT, 128...  36 us
    pallas_call x1, Pallas kernels, on_device(): pl.pallas_call(finish, out_shape=jax.ShapeDtypeStruct((BANDS, CUT, 128),...  1.92 us

profile of v7, /device:TPU:100, one launch (start us, length us, event | category | flops | bytes accessed | tf_op | source)
XLA Modules:
  0.0 37.9 jit_solution(12251283772906681364)
XLA Ops:
  0.0 36.0 %shard_map.100 = (bf16[32,64,128]{2,1,0:T(8,128)(2,1)}, bf16[2,64,128]{2,1,0:T(8,128)(2,1)}) custom-call(f32[6,64,128]{2,1,0:T(8,128)} %bitcast.19, bf16[16,256,128]{2,1,0:T(8,128)(2,1)} %bitcast.18, f32[1,128]{1,0:T(1,128)} %weights_h.1, s32[1,128]{1,0:T(1,128)} %coverage_h.1, s32[2,128]{1,0:T(2,128)} %bitcast.21, bf16[1,4096]{1,0:T(2,128)(2,1)} %psf_y_h.1, ...), custom_call_target="tpu_custom_call" | custom-call | tf_op jit(solution)/shard_map/pallas_call | solution.py:397
  36.0 1.9 %shard_map.101 = f32[6,64,128]{2,1,0:T(8,128)} custom-call(f32[6,64,128]{2,1,0:T(8,128)} %bitcast.20, bf16[32,64,128]{2,1,0:T(8,128)(2,1)} %get-tuple-element.7.terms_h, bf16[2,64,128]{2,1,0:T(8,128)(2,1)} %get-tuple-element.8.terms2_h, s32[1,2]{1,0:T(1,128)} %counts_h.1), custom_call_target="tpu_custom_call" | custom-call | tf_op jit(solution)/shard_map/pallas_call | solution.py:446
